TPU v7x, 512 devices: a whole 4x8x8 slice. The times are simulated.
512 devices in a mesh: dp: 8 (over y_hi, core), expert: 64 (over y_lo, x, z).
Axes of the slice: x: 4, y: 8 (y_hi: 4, y_lo: 2; y = y_hi * 2 + y_lo), z: 8, core: 2. Of those that a mesh axis runs over, the one named last changes fastest.
Arguments:
- weights: bfloat16 [16, 3584, 512], P(None, ('dp', 'expert')), may hold values from -0.09375 to 0.09375
- first_moment: float32 [16, 3584, 512], P(None, ('dp', 'expert')), may hold values from -3 to 3
- second_moment: float32 [16, 3584, 512], P(None, ('dp', 'expert')), may hold values from 0.05 to 2
- placement: int32 [64], replicated, may hold values from 0 to 15, as said below
- block_counts: int32 [8, 64], P('dp', 'expert'), may hold values from 1 to 2
- tokens: bfloat16 [8, 64, 256, 3584], P('dp', 'expert'), may hold values from -6 to 6
- hidden_grad: bfloat16 [8, 64, 256, 256], P('dp', 'expert'), may hold values from -1.1953125 to 1.1953125
Outputs:
- new_weights: bfloat16 [64, 3584, 512], P('expert', 'dp')
- new_first: float32 [64, 3584, 512], P('expert', 'dp')
- new_second: float32 [64, 3584, 512], P('expert', 'dp')
Inputs may be any that keep to these rules, and one draw needn't show every extreme that they name: `placement`: every expert block 0 to 15 is owned by at least one device. `block_counts`: the rows after a device's live blocks are padding.
All inputs are finite; a program needn't handle non-finite values.
Results may differ from a plain program's by a relative error of at most 0.015.
Values may be sent and summed in bfloat16 or wider, within the bound.
No kernel may reach another device: no remote copies, remote signals or barrier semaphores. Data moves between devices by JAX's collectives and lax.ppermute only.
A program may use at most 64 MiB of HBM per device.

v0:
```python
import jax
import jax.numpy as jnp
from jax import lax
from jax.sharding import PartitionSpec as P

BLOCK = 128
beta_first = 0.9
beta_second = 0.95
learning_rate = 0.001
weight_decay = 0.1
adam_epsilon = 1e-08
adam_steps = 10.0


def silu_grads(projected, upstream, live_mask):
    half_width = projected.shape[1] // 2
    gate_part = projected[:, :half_width]
    upward = projected[:, half_width:]
    sigmoid_gate = jax.nn.sigmoid(gate_part)
    masked = jnp.where(live_mask, upstream.astype(jnp.float32), 0.0)
    grad_gate = masked * upward * sigmoid_gate * (1.0 + gate_part * (1.0 - sigmoid_gate))
    grad_upward = masked * gate_part * sigmoid_gate
    return jnp.concatenate([grad_gate, grad_upward], axis=1).astype(jnp.bfloat16)


def adam_update(params, first_moment, second_moment, gradient):
    moment_one = beta_first * first_moment + (1.0 - beta_first) * gradient
    moment_two = beta_second * second_moment + (1.0 - beta_second) * gradient * gradient
    correct_one = 1.0 - beta_first**adam_steps
    correct_two = 1.0 - beta_second**adam_steps
    params_full = params.astype(jnp.float32)
    step_size = (
        moment_one / correct_one / (jnp.sqrt(moment_two / correct_two) + adam_epsilon)
        + weight_decay * params_full
    )
    return ((params_full - learning_rate * step_size).astype(jnp.bfloat16), moment_one, moment_two)


def on_device(weights, first_moment, second_moment, placement, block_counts, tokens, hidden_grad):
    expert_count = lax.axis_size("expert")
    block_total = weights.shape[0]
    span_rows = weights.shape[1]
    col_total = weights.shape[2]
    inputs = tokens[0, 0]
    row_total = inputs.shape[0]
    narrow = jnp.bfloat16
    live_mask = (jnp.arange(row_total) < BLOCK * block_counts[0, 0])[:, None]
    own_shape = (expert_count * span_rows, col_total)
    pick = (placement[:, None] == jnp.arange(block_total)[None, :]).astype(narrow)
    same = (placement[:, None] == placement[None, :]).astype(narrow)

    def exchange(values):
        return lax.all_to_all(values, "expert", split_axis=0, concat_axis=0, tiled=True)

    def spread(stored):
        return jnp.einsum("ju,urc->jrc", pick, stored, preferred_element_type=jnp.float32).astype(
            narrow
        )

    arrived = exchange(spread(weights))
    own_rows = arrived.reshape(own_shape)
    gathered = lax.all_gather(own_rows, "dp", axis=0, tiled=True)
    moments = jnp.concatenate([first_moment, second_moment], axis=1).astype(narrow)
    moments_sent, _ = lax.optimization_barrier((spread(moments), arrived))
    moments_here = exchange(moments_sent)
    gathered, moments_here = lax.optimization_barrier((gathered, moments_here))
    projected = jnp.dot(inputs, gathered, preferred_element_type=jnp.float32)
    grad_proj = silu_grads(projected, hidden_grad[0, 0], live_mask)
    term = lax.dot_general(
        inputs, grad_proj, (((0,), (0,)), ((), ())), preferred_element_type=jnp.float32
    ).astype(narrow)
    summed_data = lax.psum_scatter(term, "dp", scatter_dimension=0, tiled=True)
    at_home = exchange(summed_data.reshape(expert_count, span_rows, col_total))
    block_grad = jnp.einsum(
        "jk,krc->jrc", same, at_home, preferred_element_type=jnp.float32
    ).astype(narrow)
    grad_here = exchange(block_grad)
    updated, moment_one, moment_two = adam_update(
        own_rows,
        moments_here[:, :span_rows].reshape(own_shape).astype(jnp.float32),
        moments_here[:, span_rows:].reshape(own_shape).astype(jnp.float32),
        grad_here.reshape(own_shape).astype(jnp.float32),
    )
    return (updated[None], moment_one[None], moment_two[None])


def solution(mesh):
    in_specs = (
        P(None, ("dp", "expert"), None),
        P(None, ("dp", "expert"), None),
        P(None, ("dp", "expert"), None),
        P(),
        P("dp", "expert"),
        P("dp", "expert", None, None),
        P("dp", "expert", None, None),
    )
    out_specs = (P("expert", "dp", None), P("expert", "dp", None), P("expert", "dp", None))
    return jax.shard_map(
        on_device, mesh=mesh, in_specs=in_specs, out_specs=out_specs, check_vma=False
    )
```

profile of v0, /device:TPU:16, one launch (start us, length us, event | category | flops | bytes accessed | tf_op | source)
XLA Modules:
  0.0 233.5 jit_solution(11896177370033334054)
XLA Ops:
  7.2 0.0 copy-start
  7.2 0.0 copy-start.4
  7.2 0.0 copy-start.2
  7.2 0.0 copy-start.3
  7.2 0.0 all-gather.2.cloned.1.call-start
  7.3 1.4 convolution_convert_fusion.2
  8.6 0.3 copy.20
  8.9 33.6 %all_to_all.20 = bf16[64,7,512]{2,1,0:T(8,128)(2,1)S(1)} all-to-all(bf16[64,7,512]{2,1,0:T(8,128)(2,1)S(1)} %copy.20), channel_id=1, replica_groups=mesh['dp'=8,'expert'=64] {'expert'}, dimensions={0} | all-to-all | bytes 917504 | tf_op jit(solution)/shard_map/all_to_all | solution.py:53
  42.5 0.9 reshape.142
  43.4 0.0 all-gather.2.cloned.1.call-update
  43.5 0.0 copy-done.2
  43.5 0.0 copy-done.3
  43.5 0.0 copy-done.4
  43.5 0.4 convolution_convert_fusion.1
  44.0 1.5 copy.21
  45.5 4.7 %all-to-all-start.1 = ((bf16[64,14,512]{2,1,0:T(8,128)(2,1)}), bf16[64,14,512]{2,1,0:T(8,128)(2,1)S(1)}, u32[]{:S(2)}, u32[]{:S(2)}) async-start(bf16[64,14,512]{2,1,0:T(8,128)(2,1)} %copy.21), calls=%async_computation.1 | async-start | bytes 2097152 | tf_op jit(solution)/shard_map/all_to_all | solution.py:53
  50.2 0.0 reduce-scatter.4.cloned.1.call-start
  50.2 1.0 copy.22
  51.9 33.5 %all-to-all-done.1 = bf16[64,14,512]{2,1,0:T(8,128)(2,1)S(1)} async-done(((bf16[64,14,512]{2,1,0:T(8,128)(2,1)}), bf16[64,14,512]{2,1,0:T(8,128)(2,1)S(1)}, u32[]{:S(2)}, u32[]{:S(2)}) %all-to-all-start.1) | async-done | bytes 917536 | tf_op jit(solution)/shard_map/all_to_all | solution.py:53
  85.4 9.9 %all-gather.2.cloned.1.call-done = bf16[3584,512]{1,0:T(8,128)(2,1)} async-done(((bf16[448,512]{1,0:T(8,128)(2,1)}), bf16[3584,512]{1,0:T(8,128)(2,1)}) %all-gather.2.cloned.1.call-update) | async-done | bytes 3670032 | tf_op jit(solution)/shard_map/all_gather | solution.py:62
  95.3 0.0 copy-done
  95.3 3.2 %fusion.4 = f32[256,512]{0,1:T(8,128)S(1)} fusion(bf16[3584,512]{1,0:T(8,128)(2,1)} %all-gather.2.cloned.1.call-done, bf16[1,1,256,3584]{3,2,1,0:T(8,128)(2,1)S(1)} %copy-done), kind=kOutput, calls=%fused_computation.9 | convolution fusion | flops 939524096 | bytes 6029312 | tf_op jit(solution)/shard_map/dot_general | solution.py:67
  98.5 0.2 fusion.11
  98.7 3.0 %fusion = bf16[3584,512]{0,1:T(8,128)(2,1)} fusion(bf16[1,1,256,3584]{3,2,1,0:T(8,128)(2,1)S(1)} %copy-done, bf16[256,256]{0,1:T(8,128)(2,1)S(1)} %get-tuple-element.15, bf16[256,256]{0,1:T(8,128)(2,1)S(1)} %get-tuple-element.14), kind=kOutput, calls=%fused_computation.1 | convolution fusion | flops 941883392 | bytes 5767168 | tf_op jit(solution)/shard_map/dot_general | solution.py:69
  101.6 6.0 %copy.26 = bf16[3584,512]{1,0:T(8,128)(2,1)} copy(bf16[3584,512]{0,1:T(8,128)(2,1)} %fusion) | data formatting | bytes 7340032
  107.6 0.0 reduce-scatter.4.cloned.1.call-update
  107.6 52.1 %reduce-scatter.4.cloned.1.call-done = bf16[448,512]{1,0:T(8,128)(2,1)} async-done(((bf16[3584,512]{1,0:T(8,128)(2,1)}), bf16[448,512]{1,0:T(8,128)(2,1)}) %reduce-scatter.4.cloned.1.call-update) | async-done | bytes 458768 | tf_op jit(solution)/shard_map/reduce_scatter | solution.py:72
  159.7 2.0 reshape.143
  161.7 31.4 %all_to_all.21 = bf16[64,7,512]{2,1,0:T(8,128)(2,1)S(1)} all-to-all(bf16[64,7,512]{2,1,0:T(8,128)(2,1)} %reshape.143), channel_id=1, replica_groups=mesh['dp'=8,'expert'=64] {'expert'}, dimensions={0} | all-to-all | bytes 917504 | tf_op jit(solution)/shard_map/all_to_all | solution.py:53
  193.1 0.3 convolution_convert_fusion.3
  193.4 1.1 copy.25
  194.5 6.6 %all-to-all-start.3 = ((bf16[64,7,512]{2,1,0:T(8,128)(2,1)}), bf16[64,7,512]{2,1,0:T(8,128)(2,1)}, u32[]{:S(2)}, u32[]{:S(2)}) async-start(bf16[64,7,512]{2,1,0:T(8,128)(2,1)} %copy.25), calls=%async_computation.3 | async-start | bytes 1048576 | tf_op jit(solution)/shard_map/all_to_all | solution.py:53
  201.0 1.1 reshape.144
  202.1 1.6 convert_multiply_fusion
  203.7 0.0 copy-start.1
  203.7 2.4 %mul.128 = f32[1,448,512]{2,1,0:T(8,128)} reshape(f32[64,7,512]{2,1,0:T(8,128)} %get-tuple-element.13) | data formatting | bytes 1835008 | tf_op jit(solution)/shard_map/mul | solution.py:27
  206.1 2.3 mul.138
  208.4 12.5 %all-to-all-done.3 = bf16[64,7,512]{2,1,0:T(8,128)(2,1)} async-done(((bf16[64,7,512]{2,1,0:T(8,128)(2,1)}), bf16[64,7,512]{2,1,0:T(8,128)(2,1)}, u32[]{:S(2)}, u32[]{:S(2)}) %all-to-all-start.3) | async-done | bytes 458784 | tf_op jit(solution)/shard_map/all_to_all | solution.py:53
  220.9 2.1 reshape.146
  223.0 0.0 copy-done.1
  223.0 3.6 %subtract_convert_fusion = (bf16[1,448,512]{2,1,0:T(8,128)(2,1)}, f32[1,448,512]{2,1,0:T(8,128)}, f32[1,448,512]{2,1,0:T(8,128)}) fusion(f32[1,448,512]{2,1,0:T(8,128)S(1)} %copy-done.1, f32[1,448,512]{2,1,0:T(8,128)} %mul.128, f32[1,448,512]{2,1,0:T(8,128)} %reshape.146, f32[1,448,512]{2,1,0:T(8,128)} %mul.138), kind=kLoop, calls=%fused_computation.13 | loop fusion | flops 3211264 | bytes 5963776 | tf_op jit(solution)/shard_map/convert_element_type | solution.py:36
  (3 shorter events, 0.0 us)
Async XLA Ops:
  7.2 88.2 %copy-start = (bf16[1,1,256,3584]{3,2,1,0:T(8,128)(2,1)S(1)}, bf16[1,1,256,3584]{3,2,1,0:T(8,128)(2,1)}, u32[]{:S(2)}) copy-start(bf16[1,1,256,3584]{3,2,1,0:T(8,128)(2,1)} %param.12) | copy-start | bytes 5505028
  7.2 36.4 %copy-start.4 = (s32[64]{0:T(128)S(1)}, s32[64]{0:T(128)}, u32[]{:S(2)}) copy-start(s32[64]{0:T(128)} %param.10) | copy-start | bytes 772
  7.2 36.3 %copy-start.2 = (f32[16,7,512]{2,0,1:T(8,128)S(1)}, f32[16,7,512]{2,0,1:T(8,128)}, u32[]{:S(2)}) copy-start(f32[16,7,512]{2,0,1:T(8,128)} %param.8) | copy-start | bytes 688132
  7.2 36.3 %copy-start.3 = (f32[16,7,512]{2,0,1:T(8,128)S(1)}, f32[16,7,512]{2,0,1:T(8,128)}, u32[]{:S(2)}) copy-start(f32[16,7,512]{2,0,1:T(8,128)} %param.9) | copy-start | bytes 688132
  7.2 88.1 %all-gather.2.cloned.1.call-start = ((), (), s32[]{:S(2)}) async-start(), calls=%async_computation.5 | async-start | bytes 4128768 | tf_op jit(solution)/shard_map/all_gather | solution.py:62
  45.5 39.9 %all-to-all-start.1 = ((bf16[64,14,512]{2,1,0:T(8,128)(2,1)}), bf16[64,14,512]{2,1,0:T(8,128)(2,1)S(1)}, u32[]{:S(2)}, u32[]{:S(2)}) async-start(bf16[64,14,512]{2,1,0:T(8,128)(2,1)} %copy.21), calls=%async_computation.1 | async-start | bytes 2097152 | tf_op jit(solution)/shard_map/all_to_all | solution.py:53
  50.2 109.5 %reduce-scatter.4.cloned.1.call-start = ((), (), s32[]{:S(2)}) async-start(), calls=%async_computation.6 | async-start | bytes 4128768 | tf_op jit(solution)/shard_map/reduce_scatter | solution.py:72
  194.5 26.5 %all-to-all-start.3 = ((bf16[64,7,512]{2,1,0:T(8,128)(2,1)}), bf16[64,7,512]{2,1,0:T(8,128)(2,1)}, u32[]{:S(2)}, u32[]{:S(2)}) async-start(bf16[64,7,512]{2,1,0:T(8,128)(2,1)} %copy.25), calls=%async_computation.3 | async-start | bytes 1048576 | tf_op jit(solution)/shard_map/all_to_all | solution.py:53
  203.7 19.3 %copy-start.1 = (f32[1,448,512]{2,1,0:T(8,128)S(1)}, f32[1,448,512]{2,1,0:T(8,128)}, u32[]{:S(2)}) copy-start(f32[1,448,512]{2,1,0:T(8,128)} %reshape.144) | copy-start | bytes 2752516
Sparse Core Ops, SparseCore 0:
  43.6 51.6 all-gather.1
  107.8 51.8 reduce-scatter.3
where the time goes:
time: 234 us; the launch traced here: 233 us
  waiting for transfers between devices  108 us (46%)
  blocking collectives  65 us (28%)
  local copies, waits for them, and re-layouts  20.5 us (9%)
  between operations  14.8 us (6%)
  starting transfers between devices  11.3 us (5%)
  matrix products  8.32 us (4%)
  other arithmetic  5.46 us (2%)
    all_to_all x2, blocking collectives, exchange(): lax.all_to_all(values, 'expert', split_axis=0, concat_axis=0, tiled=True)  65 us
    reduce_scatter x1, waiting for transfers between devices, on_device(): summed_data = lax.psum_scatter(term, 'dp', scatter_dimension=0, tiled=True)  52.1 us
    all_to_all x2, waiting for transfers between devices, exchange(): lax.all_to_all(values, 'expert', split_axis=0, concat_axis=0, tiled=True)  46 us
    all_to_all x2, starting transfers between devices, exchange(): lax.all_to_all(values, 'expert', split_axis=0, concat_axis=0, tiled=True)  11.2 us
    all_gather x1, waiting for transfers between devices, on_device(): gathered = lax.all_gather(own_rows, 'dp', axis=0, tiled=True)  9.94 us
    unnamed x12, local copies, waits for them, and re-layouts  7.01 us
  transfers between devices with their start and end apart: 4, of which 4 were waited for; matrix products, arithmetic and copies ran while one was open for 4% of the time, Pallas kernels for 0%

commit v1 on v0

--- a/solution.py
+++ b/solution.py
@@ -59,7 +59,8 @@
 
     arrived = exchange(spread(weights))
     own_rows = arrived.reshape(own_shape)
-    gathered = lax.all_gather(own_rows, "dp", axis=0, tiled=True)
+    repeated = jnp.stack([own_rows] * lax.axis_size("dp"))
+    gathered = jnp.concatenate(lax.all_to_all(repeated, "dp", 0, 0), axis=0)
     moments = jnp.concatenate([first_moment, second_moment], axis=1).astype(narrow)
     moments_sent, _ = lax.optimization_barrier((spread(moments), arrived))
     moments_here = exchange(moments_sent)

time: 234 us -> 305 us (1.30)
  waiting for transfers between devices: 108 us -> 184 us
  blocking collectives: 65 us -> 31.4 us
  starting transfers between devices: 11.3 us -> 32.6 us
  local copies, waits for them, and re-layouts: 20.5 us -> 24.5 us
    all_to_all x0 -> x1, waiting for transfers between devices: none -> 81.8 us  [on_device(): gathered = jnp.concatenate(lax.all_to_all(repeated, 'dp', 0, 0), axis=0)]
    all_to_all x2 -> x1, blocking collectives: 65 us -> 31.4 us  [exchange(): lax.all_to_all(values, 'expert', split_axis=0, concat_axis=0, tiled=True)]
    all_to_all x2 -> x3, starting transfers between devices: 11.2 us -> 26.1 us  [exchange(): lax.all_to_all(values, 'expert', split_axis=0, concat_axis=0, tiled=True)]
    all_to_all x2 -> x3, waiting for transfers between devices: 46 us -> 57.6 us  [exchange(): lax.all_to_all(values, 'expert', split_axis=0, concat_axis=0, tiled=True)]
    all_gather x1 -> x0, waiting for transfers between devices: 9.94 us -> none  [on_device(): gathered = lax.all_gather(own_rows, 'dp', axis=0, tiled=True)]
    reduce_scatter x1, waiting for transfers between devices: 52.1 us -> 44.9 us  [on_device(): summed_data = lax.psum_scatter(term, 'dp', scatter_dimension=0, tiled=True)]
    all_to_all x0 -> x1, starting transfers between devices: none -> 6.53 us  [on_device(): gathered = jnp.concatenate(lax.all_to_all(repeated, 'dp', 0, 0), axis=0)]
    another operation x0 -> x2, local copies, waits for them, and re-layouts: none -> 4.09 us  [on_device(): repeated = jnp.stack([own_rows] * lax.axis_size('dp'))]
  transfers between devices with their start and end apart: 4 -> 5, of which waited for: 4 -> 5; matrix products, arithmetic and copies ran while one was open for 4% -> 4% of each run, Pallas kernels for 0% -> 0%
where the time goes in v1:
time: 305 us; the launch traced here: 304 us
  waiting for transfers between devices  184 us (60%)
  starting transfers between devices  32.6 us (11%)
  blocking collectives  31.4 us (10%)
  local copies, waits for them, and re-layouts  24.5 us (8%)
  between operations  14.8 us (5%)
  matrix products  8.93 us (3%)
  other arithmetic  7.32 us (2%)
    all_to_all x1, waiting for transfers between devices, on_device(): gathered = jnp.concatenate(lax.all_to_all(repeated, 'dp', 0, 0), axis=0)  81.8 us
    all_to_all x3, waiting for transfers between devices, exchange(): lax.all_to_all(values, 'expert', split_axis=0, concat_axis=0, tiled=True)  57.6 us
    reduce_scatter x1, waiting for transfers between devices, on_device(): summed_data = lax.psum_scatter(term, 'dp', scatter_dimension=0, tiled=True)  44.9 us
    all_to_all x1, blocking collectives, exchange(): lax.all_to_all(values, 'expert', split_axis=0, concat_axis=0, tiled=True)  31.4 us
    all_to_all x3, starting transfers between devices, exchange(): lax.all_to_all(values, 'expert', split_axis=0, concat_axis=0, tiled=True)  26.1 us
    unnamed x8, local copies, waits for them, and re-layouts  6.99 us
    all_to_all x1, starting transfers between devices, on_device(): gathered = jnp.concatenate(lax.all_to_all(repeated, 'dp', 0, 0), axis=0)  6.53 us
  transfers between devices with their start and end apart: 5, of which 5 were waited for; matrix products, arithmetic and copies ran while one was open for 4% of the time, Pallas kernels for 0%

profile of v1, /device:TPU:16, one launch (start us, length us, event | category | flops | bytes accessed | tf_op | source)
XLA Modules:
  0.0 303.7 jit_solution(15244670176033276123)
XLA Ops:
  7.2 0.0 copy-start
  7.2 1.4 convolution_convert_fusion.2
  8.6 1.1 copy.20
  9.6 14.8 %all-to-all-start = ((bf16[64,7,512]{2,1,0:T(8,128)(2,1)}), bf16[64,7,512]{2,1,0:T(8,128)(2,1)S(1)}, u32[]{:S(2)}, u32[]{:S(2)}) async-start(bf16[64,7,512]{2,1,0:T(8,128)(2,1)} %copy.20), calls=%async_computation | async-start | bytes 1048576 | tf_op jit(solution)/shard_map/all_to_all | solution.py:53
  24.4 1.0 convert.15
  25.4 1.0 convert.16
  26.3 1.1 convolution_convert_fusion.1
  27.4 16.0 %all-to-all-done = bf16[64,7,512]{2,1,0:T(8,128)(2,1)S(1)} async-done(((bf16[64,7,512]{2,1,0:T(8,128)(2,1)}), bf16[64,7,512]{2,1,0:T(8,128)(2,1)S(1)}, u32[]{:S(2)}, u32[]{:S(2)}) %all-to-all-start) | async-done | bytes 458784 | tf_op jit(solution)/shard_map/all_to_all | solution.py:53
  43.4 1.5 copy.21
  44.9 4.7 %all-to-all-start.2 = ((bf16[64,14,512]{2,1,0:T(8,128)(2,1)}), bf16[64,14,512]{2,1,0:T(8,128)(2,1)S(1)}, u32[]{:S(2)}, u32[]{:S(2)}) async-start(bf16[64,14,512]{2,1,0:T(8,128)(2,1)} %copy.21), calls=%async_computation.2 | async-start | bytes 2097152 | tf_op jit(solution)/shard_map/all_to_all | solution.py:53
  49.6 0.9 stack_reshape.2
  50.5 29.1 %all-to-all-done.2 = bf16[64,14,512]{2,1,0:T(8,128)(2,1)S(1)} async-done(((bf16[64,14,512]{2,1,0:T(8,128)(2,1)}), bf16[64,14,512]{2,1,0:T(8,128)(2,1)S(1)}, u32[]{:S(2)}, u32[]{:S(2)}) %all-to-all-start.2) | async-done | bytes 917536 | tf_op jit(solution)/shard_map/all_to_all | solution.py:53
  79.6 3.2 %stack.3 = bf16[8,448,512]{2,1,0:T(8,128)(2,1)} broadcast(bf16[448,512]{1,0:T(8,128)(2,1)} %stack_reshape.2), dimensions={1,2} | broadcast | bytes 4128768 | tf_op jit(solution)/shard_map/stack | solution.py:62
  82.8 6.5 %all-to-all-start.1 = ((bf16[8,448,512]{2,1,0:T(8,128)(2,1)}), bf16[8,448,512]{2,1,0:T(8,128)(2,1)}, u32[]{:S(2)}, u32[]{:S(2)}) async-start(bf16[8,448,512]{2,1,0:T(8,128)(2,1)} %stack.3), calls=%async_computation.1 | async-start | bytes 7340032 | tf_op jit(solution)/shard_map/all_to_all | solution.py:63
  89.3 0.0 reduce-scatter.4.cloned.1.call-start
  89.3 1.0 copy.22
  91.0 81.8 %all-to-all-done.1 = bf16[8,448,512]{2,1,0:T(8,128)(2,1)} async-done(((bf16[8,448,512]{2,1,0:T(8,128)(2,1)}), bf16[8,448,512]{2,1,0:T(8,128)(2,1)}, u32[]{:S(2)}, u32[]{:S(2)}) %all-to-all-start.1) | async-done | bytes 3670048 | tf_op jit(solution)/shard_map/all_to_all | solution.py:63
  172.7 0.0 copy-done
  172.7 3.2 %fusion.4 = f32[256,512]{0,1:T(8,128)S(1)} fusion(bf16[3584,512]{1,0:T(8,128)(2,1)} %bitcast.1, bf16[1,1,256,3584]{3,2,1,0:T(8,128)(2,1)S(1)} %copy-done), kind=kOutput, calls=%fused_computation.9 | convolution fusion | flops 939524096 | bytes 6029312 | tf_op jit(solution)/shard_map/dot_general | solution.py:68
  175.9 0.2 fusion.11
  176.1 3.0 fusion
  179.0 6.0 %copy.26 = bf16[3584,512]{1,0:T(8,128)(2,1)} copy(bf16[3584,512]{0,1:T(8,128)(2,1)} %fusion) | data formatting | bytes 7340032
  185.0 0.0 copy-start.2
  185.0 0.0 reduce-scatter.4.cloned.1.call-update
  185.0 44.9 %reduce-scatter.4.cloned.1.call-done = bf16[448,512]{1,0:T(8,128)(2,1)} async-done(((bf16[3584,512]{1,0:T(8,128)(2,1)}), bf16[448,512]{1,0:T(8,128)(2,1)}) %reduce-scatter.4.cloned.1.call-update) | async-done | bytes 458768 | tf_op jit(solution)/shard_map/reduce_scatter | solution.py:73
  229.9 2.0 reshape.146
  231.9 31.4 %all_to_all.25 = bf16[64,7,512]{2,1,0:T(8,128)(2,1)S(1)} all-to-all(bf16[64,7,512]{2,1,0:T(8,128)(2,1)} %reshape.146), channel_id=1, replica_groups=mesh['dp'=8,'expert'=64] {'expert'}, dimensions={0} | all-to-all | bytes 917504 | tf_op jit(solution)/shard_map/all_to_all | solution.py:53
  263.2 0.0 copy-done.2
  263.2 0.3 convolution_convert_fusion.3
  263.6 1.1 copy.25
  264.6 6.6 %all-to-all-start.4 = ((bf16[64,7,512]{2,1,0:T(8,128)(2,1)}), bf16[64,7,512]{2,1,0:T(8,128)(2,1)}, u32[]{:S(2)}, u32[]{:S(2)}) async-start(bf16[64,7,512]{2,1,0:T(8,128)(2,1)} %copy.25), calls=%async_computation.4 | async-start | bytes 1048576 | tf_op jit(solution)/shard_map/all_to_all | solution.py:53
  271.2 1.1 reshape.147
  272.3 1.6 convert_multiply_fusion
  273.9 0.0 copy-start.1
  273.9 2.4 mul.128
  276.3 2.3 mul.138
  278.6 12.5 %all-to-all-done.4 = bf16[64,7,512]{2,1,0:T(8,128)(2,1)} async-done(((bf16[64,7,512]{2,1,0:T(8,128)(2,1)}), bf16[64,7,512]{2,1,0:T(8,128)(2,1)}, u32[]{:S(2)}, u32[]{:S(2)}) %all-to-all-start.4) | async-done | bytes 458784 | tf_op jit(solution)/shard_map/all_to_all | solution.py:53
  291.1 2.1 reshape.149
  293.2 0.0 copy-done.1
  293.2 3.6 %subtract_convert_fusion = (bf16[1,448,512]{2,1,0:T(8,128)(2,1)}, f32[1,448,512]{2,1,0:T(8,128)}, f32[1,448,512]{2,1,0:T(8,128)}) fusion(f32[1,448,512]{2,1,0:T(8,128)S(1)} %copy-done.1, f32[1,448,512]{2,1,0:T(8,128)} %mul.128, f32[1,448,512]{2,1,0:T(8,128)} %reshape.149, f32[1,448,512]{2,1,0:T(8,128)} %mul.138), kind=kLoop, calls=%fused_computation.13 | loop fusion | flops 3211264 | bytes 5963776 | tf_op jit(solution)/shard_map/convert_element_type | solution.py:36
  (1 shorter events, 0.0 us)
Async XLA Ops:
  7.2 165.6 %copy-start = (bf16[1,1,256,3584]{3,2,1,0:T(8,128)(2,1)S(1)}, bf16[1,1,256,3584]{3,2,1,0:T(8,128)(2,1)}, u32[]{:S(2)}) copy-start(bf16[1,1,256,3584]{3,2,1,0:T(8,128)(2,1)} %param.12) | copy-start | bytes 5505028
  9.6 33.8 %all-to-all-start = ((bf16[64,7,512]{2,1,0:T(8,128)(2,1)}), bf16[64,7,512]{2,1,0:T(8,128)(2,1)S(1)}, u32[]{:S(2)}, u32[]{:S(2)}) async-start(bf16[64,7,512]{2,1,0:T(8,128)(2,1)} %copy.20), calls=%async_computation | async-start | bytes 1048576 | tf_op jit(solution)/shard_map/all_to_all | solution.py:53
  44.9 34.7 %all-to-all-start.2 = ((bf16[64,14,512]{2,1,0:T(8,128)(2,1)}), bf16[64,14,512]{2,1,0:T(8,128)(2,1)S(1)}, u32[]{:S(2)}, u32[]{:S(2)}) async-start(bf16[64,14,512]{2,1,0:T(8,128)(2,1)} %copy.21), calls=%async_computation.2 | async-start | bytes 2097152 | tf_op jit(solution)/shard_map/all_to_all | solution.py:53
  82.8 90.0 %all-to-all-start.1 = ((bf16[8,448,512]{2,1,0:T(8,128)(2,1)}), bf16[8,448,512]{2,1,0:T(8,128)(2,1)}, u32[]{:S(2)}, u32[]{:S(2)}) async-start(bf16[8,448,512]{2,1,0:T(8,128)(2,1)} %stack.3), calls=%async_computation.1 | async-start | bytes 7340032 | tf_op jit(solution)/shard_map/all_to_all | solution.py:63
  89.3 140.6 %reduce-scatter.4.cloned.1.call-start = ((), (), s32[]{:S(2)}) async-start(), calls=%async_computation.6 | async-start | bytes 4128768 | tf_op jit(solution)/shard_map/reduce_scatter | solution.py:73
  185.0 78.2 %copy-start.2 = (s32[64]{0:T(128)S(1)}, s32[64]{0:T(128)}, u32[]{:S(2)}) copy-start(s32[64]{0:T(128)} %param.10) | copy-start | bytes 772
  264.6 26.5 %all-to-all-start.4 = ((bf16[64,7,512]{2,1,0:T(8,128)(2,1)}), bf16[64,7,512]{2,1,0:T(8,128)(2,1)}, u32[]{:S(2)}, u32[]{:S(2)}) async-start(bf16[64,7,512]{2,1,0:T(8,128)(2,1)} %copy.25), calls=%async_computation.4 | async-start | bytes 1048576 | tf_op jit(solution)/shard_map/all_to_all | solution.py:53
  273.9 19.3 %copy-start.1 = (f32[1,448,512]{2,1,0:T(8,128)S(1)}, f32[1,448,512]{2,1,0:T(8,128)}, u32[]{:S(2)}) copy-start(f32[1,448,512]{2,1,0:T(8,128)} %reshape.147) | copy-start | bytes 2752516
Sparse Core Ops, SparseCore 0:
  185.2 44.6 reduce-scatter.3
